TPU v7x, 32 devices: a whole 2x2x4 slice. The times are simulated.
32 devices in a mesh: mod: 4 (over y, x), seq: 8 (over z, core).
Axes of the slice: x: 2, y: 2, z: 4, core: 2. Of those that a mesh axis runs over, the one named last changes fastest.
Arguments:
- tokens: bfloat16 [2048, 4096], P(('mod', 'seq')), may hold values from -6 to 6
- norm_gain: float32 [3, 4096], replicated, may hold values from 0.2 to 2.6
- qkv_weight: bfloat16 [3, 4096, 12288], P(None, None, 'seq'), may hold values from -0.45 to 0.45
- out_weight: bfloat16 [3, 4096, 4096], P(None, 'seq'), may hold values from -0.375 to 0.375
- modality: int32 [16], replicated, may hold values from 0 to 2
- doc_lengths: int32 [4], replicated, may hold values from 1 to 1024, 2048 in all
Outputs:
- mixed: bfloat16 [2048, 4096], P(('mod', 'seq'))
Inputs may be any that keep to these rules, and one draw needn't show every extreme that they name: `doc_lengths`: the lengths sum to 2048; documents follow one another from position 0 in the given order.
All inputs are finite; a program needn't handle non-finite values.
Results may differ from a plain program's by a relative error of at most 0.015.
Values may be sent and summed in bfloat16 or wider, within the bound.
A program may use at most 128 MiB of HBM per device.

v0:
```python
import math
import jax
import jax.numpy as jnp
from jax import lax
from jax.sharding import PartitionSpec as P

HDIM = 128
BLOCK = 128


def modes_of_rows(first_row, row_count, modality):
    block_ids = (first_row + jnp.arange(row_count, dtype=jnp.int32)) // BLOCK
    block_table = jnp.arange(modality.shape[0], dtype=jnp.int32)
    picked = jnp.where(block_ids[:, None] == block_table[None, :], modality[None, :], 0)
    return jnp.sum(picked, axis=1)


def documents(positions, doc_lengths):
    doc_ends = jnp.cumsum(doc_lengths)
    return jnp.sum((positions[:, None] >= doc_ends[None, :]).astype(jnp.int32), axis=1)


def body(tokens, norm_gain, qkv_weight, out_weight, modality, doc_lengths):
    row_count = tokens.shape[0]
    seq_count = lax.axis_size("seq")
    mod_count = lax.axis_size("mod")
    group_rows = row_count * seq_count
    mod_index = lax.axis_index("mod")
    own_first = (mod_index * seq_count + lax.axis_index("seq")) * row_count
    row_modes = modes_of_rows(own_first, row_count, modality)
    choose = (
        row_modes[:, None, None] == jnp.arange(norm_gain.shape[0], dtype=jnp.int32)[None, :, None]
    )
    gain_rows = jnp.sum(jnp.where(choose, norm_gain[None, :, :], 0.0), axis=1)
    values = tokens.astype(jnp.float32)
    mean_square = jnp.mean(values * values, axis=1, keepdims=True)
    normed = (values * lax.rsqrt(mean_square + 1e-05) * gain_rows).astype(jnp.bfloat16)
    gathered = lax.all_gather(normed, "seq", axis=0, tiled=True)
    group_first = mod_index * group_rows
    block_count = group_rows // BLOCK
    block_modes = lax.dynamic_slice_in_dim(modality, group_first // BLOCK, block_count)
    heads_here = qkv_weight.shape[2] // (3 * HDIM)

    def project(block_pair):
        row_block, block_mode = block_pair
        weight = lax.dynamic_index_in_dim(qkv_weight, block_mode, 0, keepdims=False)
        return jnp.dot(row_block, weight, preferred_element_type=jnp.float32).astype(jnp.bfloat16)

    projected = lax.map(
        project, (gathered.reshape(block_count, BLOCK, gathered.shape[1]), block_modes)
    )
    projected = projected.reshape(group_rows, heads_here, 3, HDIM)
    queries = projected[:, :, 0, :]
    keys_here = projected[:, :, 1, :]
    values_here = projected[:, :, 2, :]
    quarter = group_rows // mod_count
    local_rows = jnp.arange(group_rows, dtype=jnp.int32)
    query_pos = group_first + local_rows
    query_docs = documents(query_pos, doc_lengths)
    block_size = min(512, quarter)
    block_total = group_rows // block_size
    score_scale = 1.0 / math.sqrt(HDIM)
    query_blocks = queries.reshape(block_total, block_size, heads_here, HDIM)
    pos_blocks = query_pos.reshape(block_total, block_size)
    doc_blocks = query_docs.reshape(block_total, block_size)
    start_state = (
        jnp.full((block_total, heads_here, block_size), -1e30, jnp.float32),
        jnp.zeros((block_total, heads_here, block_size), jnp.float32),
        jnp.zeros((block_total, block_size, heads_here, HDIM), jnp.float32),
    )
    key_start = jnp.int32(0)
    piece_keys = lax.all_gather(keys_here, "mod", axis=0, tiled=True)
    piece_values = lax.all_gather(values_here, "mod", axis=0, tiled=True)
    key_count = piece_keys.shape[0]
    key_pos = jnp.arange(key_count, dtype=jnp.int32)
    key_docs = documents(key_pos, doc_lengths)

    def one_block(block_state):
        row_max, totals, summed_rows, query_block, block_pos, block_docs = block_state

        def attend(unused):
            scores = (
                jnp.einsum(
                    "qhc,khc->hqk", query_block, piece_keys, preferred_element_type=jnp.float32
                )
                * score_scale
            )
            allowed = (
                (key_pos[None, :] <= block_pos[:, None])
                & (key_docs[None, :] == block_docs[:, None])
            )[None, :, :]
            new_max = jnp.maximum(row_max, jnp.max(jnp.where(allowed, scores, -1e30), axis=2))
            weights = jnp.where(allowed, jnp.exp(scores - new_max[:, :, None]), 0.0)
            rescale = jnp.exp(row_max - new_max)
            new_totals = totals * rescale + jnp.sum(weights, axis=2)
            added_rows = jnp.einsum(
                "hqk,khc->qhc",
                weights.astype(jnp.bfloat16),
                piece_values,
                preferred_element_type=jnp.float32,
            )
            new_rows = summed_rows * jnp.transpose(rescale)[:, :, None] + added_rows
            return (new_max, new_totals, new_rows)

        def keep_state(unused):
            return (row_max, totals, summed_rows)

        return lax.cond(key_start <= jnp.max(block_pos), attend, keep_state, 0)

    row_max, totals, summed_rows = lax.map(
        one_block,
        (start_state[0], start_state[1], start_state[2], query_blocks, pos_blocks, doc_blocks),
    )
    divisor = jnp.transpose(totals, (0, 2, 1))[:, :, :, None]
    attended = (summed_rows / divisor).astype(jnp.bfloat16).reshape(group_rows, heads_here * HDIM)

    def output(block_pair):
        row_block, block_mode = block_pair
        weight = lax.dynamic_index_in_dim(out_weight, block_mode, 0, keepdims=False)
        return jnp.dot(row_block, weight, preferred_element_type=jnp.float32)

    partial_value = lax.map(
        output, (attended.reshape(block_count, BLOCK, attended.shape[1]), block_modes)
    )
    head_sums = lax.psum_scatter(
        partial_value.reshape(group_rows, partial_value.shape[2]).astype(jnp.bfloat16),
        "seq",
        scatter_dimension=0,
        tiled=True,
    ).astype(jnp.float32)
    return (tokens.astype(jnp.float32) + head_sums).astype(jnp.bfloat16)


def solution(mesh):
    return jax.shard_map(
        body,
        mesh=mesh,
        in_specs=(
            P(("mod", "seq"), None),
            P(),
            P(None, None, "seq"),
            P(None, "seq", None),
            P(),
            P(),
        ),
        out_specs=P(("mod", "seq"), None),
        check_vma=False,
    )
```

profile of v0, /device:TPU:0, one launch (start us, length us, event | category | flops | bytes accessed | tf_op | source)
XLA Modules:
  0.0 286.2 jit_solution(8059738032792153300)
XLA Ops:
  6.6 0.8 select_reduce_fusion.2
  7.4 1.2 fusion.48
  8.6 1.3 select_reduce_fusion.1
  9.9 2.0 fusion.50
  12.2 49.6 %all-gather.6.cloned.1.call-done = bf16[512,4096]{1,0:T(8,128)(2,1)} async-done(((bf16[64,4096]{1,0:T(8,128)(2,1)}), bf16[512,4096]{1,0:T(8,128)(2,1)}) %all-gather.6.cloned.1.call-update) | async-done | bytes 4194320 | tf_op jit(solution)/shard_map/all_gather | solution.py:38
  61.7 37.1 %while.33 = (s32[]{:T(128)}, bf16[4,128,1536]{2,1,0:T(8,128)(2,1)S(1)}, bf16[4,128,4096]{2,1,0:T(8,128)(2,1)}, s32[4]{0:T(128)S(1)}, bf16[3,4096,1536]{2,1,0:T(8,128)(2,1)}, /*index=5*/s32[]{:T(128)}, s32[]{:T(128)}, s32[]{:T(128)}) while((s32[]{:T(128)}, bf16[4,128,1536]{2,1,0:T(8,128)(2,1)S(1)}, bf16[4,128,4096]{2,1,0:T(8,128)(2,1)}, ...), condition=%wide.region_4.5_spmd, body=%wide.region_3.4_spmd.sunk | while | flops 1610809344 | bytes 14025863 | solution.py:49
  61.7 0.6 dynamic_slice.95
  64.3 6.7 %fusion.65 = bf16[4,128,1536]{2,1,0:T(8,128)(2,1)S(1)} fusion(bf16[4,128,1536]{2,1,0:T(8,128)(2,1)S(1)} %get-tuple-element.457, s32[]{:T(128)} %get-tuple-element.456, bf16[3,4096,1536]{2,1,0:T(8,128)(2,1)} %get-tuple-element.468, s32[]{:T(128)S(6)} %select_n.67, bf16[4,128,4096]{2,1,0:T(8,128)(2,1)} %get-tuple-element.466), kind=kOutput, calls=%fused_computation.6.clone.1 | convolution fusion | flops 1610809344 | bytes 14025732 | tf_op jit(solution)/shard_map/while/body/eval_jaxpr/dot_general | solution.py:47
  71.0 0.6 dynamic_slice.95
  73.5 6.7 %fusion.65 = bf16[4,128,1536]{2,1,0:T(8,128)(2,1)S(1)} fusion(bf16[4,128,1536]{2,1,0:T(8,128)(2,1)S(1)} %get-tuple-element.457, s32[]{:T(128)} %get-tuple-element.456, bf16[3,4096,1536]{2,1,0:T(8,128)(2,1)} %get-tuple-element.468, s32[]{:T(128)S(6)} %select_n.67, bf16[4,128,4096]{2,1,0:T(8,128)(2,1)} %get-tuple-element.466), kind=kOutput, calls=%fused_computation.6.clone.1 | convolution fusion | flops 1610809344 | bytes 14025732 | tf_op jit(solution)/shard_map/while/body/eval_jaxpr/dot_general | solution.py:47
  80.3 0.6 dynamic_slice.95
  82.8 6.7 %fusion.65 = bf16[4,128,1536]{2,1,0:T(8,128)(2,1)S(1)} fusion(bf16[4,128,1536]{2,1,0:T(8,128)(2,1)S(1)} %get-tuple-element.457, s32[]{:T(128)} %get-tuple-element.456, bf16[3,4096,1536]{2,1,0:T(8,128)(2,1)} %get-tuple-element.468, s32[]{:T(128)S(6)} %select_n.67, bf16[4,128,4096]{2,1,0:T(8,128)(2,1)} %get-tuple-element.466), kind=kOutput, calls=%fused_computation.6.clone.1 | convolution fusion | flops 1610809344 | bytes 14025732 | tf_op jit(solution)/shard_map/while/body/eval_jaxpr/dot_general | solution.py:47
  89.5 0.6 dynamic_slice.95
  92.1 6.7 %fusion.65 = bf16[4,128,1536]{2,1,0:T(8,128)(2,1)S(1)} fusion(bf16[4,128,1536]{2,1,0:T(8,128)(2,1)S(1)} %get-tuple-element.457, s32[]{:T(128)} %get-tuple-element.456, bf16[3,4096,1536]{2,1,0:T(8,128)(2,1)} %get-tuple-element.468, s32[]{:T(128)S(6)} %select_n.67, bf16[4,128,4096]{2,1,0:T(8,128)(2,1)} %get-tuple-element.466), kind=kOutput, calls=%fused_computation.6.clone.1 | convolution fusion | flops 1610809344 | bytes 14025732 | tf_op jit(solution)/shard_map/while/body/eval_jaxpr/dot_general | solution.py:47
  98.8 1.1 copy.14
  99.9 0.6 reshape.161
  100.6 1.1 fusion.53
  101.8 0.7 all-gather.10.cloned.1.call-update
  102.9 0.3 copy.15
  103.3 32.5 %all-gather.8.cloned.1.call-done = bf16[2048,4,1,128]{0,3,2,1:T(8,128)(2,1)} async-done(((bf16[512,4,1,128]{0,3,2,1:T(8,128)(2,1)}), bf16[2048,4,1,128]{0,3,2,1:T(8,128)(2,1)}) %all-gather.8.cloned.1.call-update) | async-done | bytes 2097168 | tf_op jit(solution)/shard_map/all_gather | solution.py:72
  135.7 3.0 %copy.17 = bf16[2048,4,128]{2,0,1:T(8,128)(2,1)S(1)} copy(bf16[2048,4,128]{0,2,1:T(8,128)(2,1)} %bitcast.85) | data formatting | bytes 4194304
  138.8 33.9 %all-gather.10.cloned.1.call-done = bf16[2048,4,1,128]{0,3,2,1:T(8,128)(2,1)} async-done(((bf16[512,4,1,128]{0,3,2,1:T(8,128)(2,1)}), bf16[2048,4,1,128]{0,3,2,1:T(8,128)(2,1)}) %all-gather.10.cloned.1.call-update) | async-done | bytes 2097168 | tf_op jit(solution)/shard_map/all_gather | solution.py:73
  172.7 4.0 %copy.18 = bf16[2048,4,128]{2,0,1:T(8,128)(2,1)} copy(bf16[2048,4,128]{0,2,1:T(8,128)(2,1)} %bitcast.86) | data formatting | bytes 4194304
  176.6 23.8 %while.35 = (s32[]{:T(128)}, f32[4,4,128]{2,1,0:T(4,128)S(1)}, f32[4,128,4,128]{1,3,2,0:T(8,128)}, s32[4,128]{1,0:T(4,128)S(1)}, s32[2048]{0:T(1024)S(1)}, /*ind...) while((s32[]{:T(128)}, f32[4,4,128]{2,1,0:T(4,128)S(1)}, ...), condition=%wide.region_14.15_spmd.clone, body=%wide.region_8.14_spmd.clone.sunk | while | flops 549324416 | bytes 28503860 | solution.py:110
  176.6 0.6 fusion.69
  178.0 3.7 %conditional.3 = (f32[1,4,128]{2,1,0:T(4,128)S(1)}, f32[1,128,4,128]{3,1,2,0:T(8,128)S(1)}) conditional(s32[]{:T(128)} %convert_element_type.82, (f32[4,128]{1,0:T(4,128)S(1)}, f32[128,4,128]{2,0,1:T(8,128)S(1)}) %tuple.105, (s32[2048]{0:T(1024)S(1)}, s32[1,128]{1,0:T(1,128)S(1)}, s32[2048]{0:T(1024)S(1)}, s32[4,128]{1,0:T(4,128)S(1)}, s32[]{:T(128)}, ...), branch_computations={%region_10.10_spmd, %region_11.13_spmd} | conditional | flops 549324288 | bytes 26912820 | solution.py:108
  178.0 0.3 compare_and_fusion
  178.3 1.0 select_reduce_fusion
  179.3 1.2 fusion.18
  180.5 1.2 fusion.31
  181.8 0.7 constant_dynamic-update-slice_fusion.5
  182.5 0.6 fusion.69
  183.9 3.7 %conditional.3 = (f32[1,4,128]{2,1,0:T(4,128)S(1)}, f32[1,128,4,128]{3,1,2,0:T(8,128)S(1)}) conditional(s32[]{:T(128)} %convert_element_type.82, (f32[4,128]{1,0:T(4,128)S(1)}, f32[128,4,128]{2,0,1:T(8,128)S(1)}) %tuple.105, (s32[2048]{0:T(1024)S(1)}, s32[1,128]{1,0:T(1,128)S(1)}, s32[2048]{0:T(1024)S(1)}, s32[4,128]{1,0:T(4,128)S(1)}, s32[]{:T(128)}, ...), branch_computations={%region_10.10_spmd, %region_11.13_spmd} | conditional | flops 549324288 | bytes 26912820 | solution.py:108
  183.9 0.3 compare_and_fusion
  184.2 1.0 select_reduce_fusion
  185.2 1.2 fusion.18
  186.4 1.2 fusion.31
  187.7 0.7 constant_dynamic-update-slice_fusion.5
  188.5 0.6 fusion.69
  189.8 3.7 %conditional.3 = (f32[1,4,128]{2,1,0:T(4,128)S(1)}, f32[1,128,4,128]{3,1,2,0:T(8,128)S(1)}) conditional(s32[]{:T(128)} %convert_element_type.82, (f32[4,128]{1,0:T(4,128)S(1)}, f32[128,4,128]{2,0,1:T(8,128)S(1)}) %tuple.105, (s32[2048]{0:T(1024)S(1)}, s32[1,128]{1,0:T(1,128)S(1)}, s32[2048]{0:T(1024)S(1)}, s32[4,128]{1,0:T(4,128)S(1)}, s32[]{:T(128)}, ...), branch_computations={%region_10.10_spmd, %region_11.13_spmd} | conditional | flops 549324288 | bytes 26912820 | solution.py:108
  189.9 0.3 compare_and_fusion
  190.2 1.0 select_reduce_fusion
  191.2 1.2 fusion.18
  192.3 1.2 fusion.31
  193.7 0.7 constant_dynamic-update-slice_fusion.5
  194.4 0.6 fusion.69
  195.8 3.7 %conditional.3 = (f32[1,4,128]{2,1,0:T(4,128)S(1)}, f32[1,128,4,128]{3,1,2,0:T(8,128)S(1)}) conditional(s32[]{:T(128)} %convert_element_type.82, (f32[4,128]{1,0:T(4,128)S(1)}, f32[128,4,128]{2,0,1:T(8,128)S(1)}) %tuple.105, (s32[2048]{0:T(1024)S(1)}, s32[1,128]{1,0:T(1,128)S(1)}, s32[2048]{0:T(1024)S(1)}, s32[4,128]{1,0:T(4,128)S(1)}, s32[]{:T(128)}, ...), branch_computations={%region_10.10_spmd, %region_11.13_spmd} | conditional | flops 549324288 | bytes 26912820 | solution.py:108
  195.8 0.3 compare_and_fusion
  196.1 1.0 select_reduce_fusion
  197.1 1.2 fusion.18
  198.3 1.2 fusion.31
  199.6 0.7 constant_dynamic-update-slice_fusion.5
  200.4 1.3 divide_convert_fusion
  201.7 25.9 %while.34 = (s32[]{:T(128)}, bf16[4,128,4096]{2,1,0:T(8,128)(2,1)}, bf16[4,128,512]{1,2,0:T(8,128)(2,1)S(1)}, s32[4]{0:T(128)S(1)}, bf16[3,512,4096]{2,1,0:T(8,128)(2,1)}, /*index=5*/s32[]{:T(128)}, s32[]{:T(128)}, s32[]{:T(128)}) while((s32[]{:T(128)}, bf16[4,128,4096]{2,1,0:T(8,128)(2,1)}, bf16[4,128,512]{1,2,0:T(8,128)(2,1)S(1)}, ...), condition=%wide.region_16.17_spmd, body=%wide.region_15.16_spmd.sunk | while | flops 536870912 | bytes 6423687 | solution.py:122
  201.7 0.6 dynamic_slice.98
  204.3 3.9 %fusion.68 = bf16[4,128,4096]{2,1,0:T(8,128)(2,1)} fusion(bf16[4,128,4096]{2,1,0:T(8,128)(2,1)} %get-tuple-element.517, s32[]{:T(128)} %get-tuple-element.516, bf16[3,512,4096]{2,1,0:T(8,128)(2,1)} %get-tuple-element.528, s32[]{:T(128)S(6)} %select_n.68, bf16[4,128,512]{1,2,0:T(8,128)(2,1)S(1)} %get-tuple-element.526), kind=kOutput, calls=%fused_computation.36.clone.1 | convolution fusion | flops 536870912 | bytes 6423556 | tf_op jit(solution)/shard_map/while/body/eval_jaxpr/dot_general | solution.py:120
  208.2 0.6 dynamic_slice.98
  210.7 4.0 %fusion.68 = bf16[4,128,4096]{2,1,0:T(8,128)(2,1)} fusion(bf16[4,128,4096]{2,1,0:T(8,128)(2,1)} %get-tuple-element.517, s32[]{:T(128)} %get-tuple-element.516, bf16[3,512,4096]{2,1,0:T(8,128)(2,1)} %get-tuple-element.528, s32[]{:T(128)S(6)} %select_n.68, bf16[4,128,512]{1,2,0:T(8,128)(2,1)S(1)} %get-tuple-element.526), kind=kOutput, calls=%fused_computation.36.clone.1 | convolution fusion | flops 536870912 | bytes 6423556 | tf_op jit(solution)/shard_map/while/body/eval_jaxpr/dot_general | solution.py:120
  214.7 0.6 dynamic_slice.98
  217.3 3.9 %fusion.68 = bf16[4,128,4096]{2,1,0:T(8,128)(2,1)} fusion(bf16[4,128,4096]{2,1,0:T(8,128)(2,1)} %get-tuple-element.517, s32[]{:T(128)} %get-tuple-element.516, bf16[3,512,4096]{2,1,0:T(8,128)(2,1)} %get-tuple-element.528, s32[]{:T(128)S(6)} %select_n.68, bf16[4,128,512]{1,2,0:T(8,128)(2,1)S(1)} %get-tuple-element.526), kind=kOutput, calls=%fused_computation.36.clone.1 | convolution fusion | flops 536870912 | bytes 6423556 | tf_op jit(solution)/shard_map/while/body/eval_jaxpr/dot_general | solution.py:120
  221.2 0.6 dynamic_slice.98
  223.7 3.9 %fusion.68 = bf16[4,128,4096]{2,1,0:T(8,128)(2,1)} fusion(bf16[4,128,4096]{2,1,0:T(8,128)(2,1)} %get-tuple-element.517, s32[]{:T(128)} %get-tuple-element.516, bf16[3,512,4096]{2,1,0:T(8,128)(2,1)} %get-tuple-element.528, s32[]{:T(128)S(6)} %select_n.68, bf16[4,128,512]{1,2,0:T(8,128)(2,1)S(1)} %get-tuple-element.526), kind=kOutput, calls=%fused_computation.36.clone.1 | convolution fusion | flops 536870912 | bytes 6423556 | tf_op jit(solution)/shard_map/while/body/eval_jaxpr/dot_general | solution.py:120
  227.7 50.1 %reduce-scatter.2.cloned.1.call-done = bf16[64,4096]{1,0:T(8,128)(2,1)} async-done(((bf16[512,4096]{1,0:T(8,128)(2,1)}), bf16[64,4096]{1,0:T(8,128)(2,1)}) %reduce-scatter.2.cloned.1.call-update) | async-done | bytes 524304 | tf_op jit(solution)/shard_map/reduce_scatter | solution.py:125
  277.8 2.0 fusion.51
  (75 shorter events, 1.6 us)
Async XLA Ops:
  6.5 5.5 %copy-start.2 = (s32[16]{0:T(128)S(1)}, s32[16]{0:T(128)}, u32[]{:S(2)}) copy-start(s32[16]{0:T(128)} %param.18) | copy-start | bytes 196
  6.5 55.2 %all-gather.6.cloned.1.call-start = ((), (), s32[]{:S(2)}) async-start(), calls=%async_computation.1 | async-start | bytes 4718592 | tf_op jit(solution)/shard_map/all_gather | solution.py:38
  12.0 123.8 %all-gather.8.cloned.1.call-start = ((), (), s32[]{:S(2)}) async-start(), calls=%async_computation.3 | async-start | bytes 2621440 | tf_op jit(solution)/shard_map/all_gather | solution.py:72
  99.9 2.6 copy-start.3
  101.7 70.9 %all-gather.10.cloned.1.call-start = ((), (), s32[]{:S(2)}) async-start(), calls=%async_computation.4 | async-start | bytes 2621440 | tf_op jit(solution)/shard_map/all_gather | solution.py:73
  102.5 175.3 %reduce-scatter.2.cloned.1.call-start = ((), (), s32[]{:S(2)}) async-start(), calls=%async_computation.2 | async-start | bytes 4718592 | tf_op jit(solution)/shard_map/reduce_scatter | solution.py:125
  178.3 2.2 copy-start.1
  184.2 2.2 copy-start.1
  190.2 2.2 copy-start.1
  196.1 2.2 copy-start.1
  227.6 50.1 %copy-start = (bf16[64,4096]{1,0:T(8,128)(2,1)S(1)}, bf16[64,4096]{1,0:T(8,128)(2,1)}, u32[]{:S(2)}) copy-start(bf16[64,4096]{1,0:T(8,128)(2,1)} %param.14) | copy-start | bytes 1572868
Sparse Core Ops, SparseCore 0:
  12.1 49.5 all-gather.5
  101.9 33.8 all-gather.7
  137.6 35.0 all-gather.9
  227.8 49.9 reduce-scatter.1
where the time goes:
time: 287 us; the launch traced here: 286 us
  waiting for transfers between devices  167 us (58%)
  matrix products  51.3 us (18%)
  local copies, waits for them, and re-layouts  18.7 us (7%)
  loops' own time  18.6 us (6%)
  other arithmetic  17.4 us (6%)
  between operations  13.3 us (5%)
    reduce_scatter x1, waiting for transfers between devices, body(): lax.psum_scatter(partial_value.reshape(group_rows, partial_value.shape[2]...  50.1 us
    all_gather x1, waiting for transfers between devices, body(): gathered = lax.all_gather(normed, 'seq', axis=0, tiled=True)  49.6 us
    all_gather x1, waiting for transfers between devices, body(): piece_values = lax.all_gather(values_here, 'mod', axis=0, tiled=True)  33.9 us
    all_gather x1, waiting for transfers between devices, body(): piece_keys = lax.all_gather(keys_here, 'mod', axis=0, tiled=True)  32.5 us
    dot_general x4, matrix products, project(): jnp.dot(row_block, weight, preferred_element_type=jnp.float32)  26.9 us
    dot_general x4, matrix products, output(): return jnp.dot(row_block, weight, preferred_element_type=jnp.float32)  15.8 us
    another operation x1, loops' own time, body(): lax.map(project, (gathered.reshape(block_count, BLOCK, gathered.shape[1])...  7.85 us
    another operation x1, loops' own time, body(): lax.map(output, (attended.reshape(block_count, BLOCK, attended.shape[1]),...  7.79 us
  transfers between devices with their start and end apart: 4, of which 4 were waited for; matrix products, arithmetic and copies ran while one was open for 1% of the time, Pallas kernels for 0%

commit v1 on v0

--- a/solution.py
+++ b/solution.py
@@ -69,7 +69,13 @@
         jnp.zeros((block_total, block_size, heads_here, HDIM), jnp.float32),
     )
     key_start = jnp.int32(0)
-    piece_keys = lax.all_gather(keys_here, "mod", axis=0, tiled=True)
+    devices = lax.axis_size("mod")
+    held, blocks = (keys_here, [keys_here])
+    for _ in range(devices - 1):
+        held = lax.ppermute(held, "mod", [(i, (i + 1) % devices) for i in range(devices)])
+        blocks.insert(0, held)
+    flat = jnp.concatenate(blocks, axis=0)
+    piece_keys = jnp.roll(flat, (lax.axis_index("mod") + 1) * keys_here.shape[0], axis=0)
     piece_values = lax.all_gather(values_here, "mod", axis=0, tiled=True)
     key_count = piece_keys.shape[0]
     key_pos = jnp.arange(key_count, dtype=jnp.int32)

time: 287 us -> 278 us (0.969)
  waiting for transfers between devices: 167 us -> 148 us
  local copies, waits for them, and re-layouts: 18.7 us -> 24.5 us
  starting transfers between devices: 0.12 us -> 3.43 us
    ppermute x0 -> x3, waiting for transfers between devices: none -> 50.1 us  [body(): lax.ppermute(held, 'mod', [(i, (i + 1) % devices) for i in range(devices)])]
    all_gather x1, waiting for transfers between devices: 33.9 us -> 0.02 us  [body(): piece_values = lax.all_gather(values_here, 'mod', axis=0, tiled=True)]
    all_gather x1 -> x0, waiting for transfers between devices: 32.5 us -> none  [body(): piece_keys = lax.all_gather(keys_here, 'mod', axis=0, tiled=True)]
    unnamed x9 -> x16, local copies, waits for them, and re-layouts: 7.05 us -> 10.6 us
    ppermute x0 -> x3, starting transfers between devices: none -> 3.34 us  [body(): lax.ppermute(held, 'mod', [(i, (i + 1) % devices) for i in range(devices)])]
  transfers between devices with their start and end apart: 4 -> 6, of which waited for: 4 -> 5; matrix products, arithmetic and copies ran while one was open for 1% -> 4% of each run, Pallas kernels for 0% -> 0%
where the time goes in v1:
time: 278 us; the launch traced here: 276 us
  waiting for transfers between devices  148 us (53%)
  matrix products  51.3 us (18%)
  local copies, waits for them, and re-layouts  24.5 us (9%)
  loops' own time  18.6 us (7%)
  other arithmetic  17.4 us (6%)
  between operations  13.3 us (5%)
  starting transfers between devices  3.43 us (1%)
    ppermute x3, waiting for transfers between devices, body(): lax.ppermute(held, 'mod', [(i, (i + 1) % devices) for i in range(devices)])  50.1 us
    all_gather x1, waiting for transfers between devices, body(): gathered = lax.all_gather(normed, 'seq', axis=0, tiled=True)  49.6 us
    reduce_scatter x1, waiting for transfers between devices, body(): lax.psum_scatter(partial_value.reshape(group_rows, partial_value.shape[2]...  48.1 us
    dot_general x4, matrix products, project(): jnp.dot(row_block, weight, preferred_element_type=jnp.float32)  26.9 us
    dot_general x4, matrix products, output(): return jnp.dot(row_block, weight, preferred_element_type=jnp.float32)  15.8 us
    unnamed x16, local copies, waits for them, and re-layouts  10.6 us
    another operation x1, loops' own time, body(): lax.map(project, (gathered.reshape(block_count, BLOCK, gathered.shape[1])...  7.85 us
    another operation x1, loops' own time, body(): lax.map(output, (attended.reshape(block_count, BLOCK, attended.shape[1]),...  7.79 us
  transfers between devices with their start and end apart: 6, of which 5 were waited for; matrix products, arithmetic and copies ran while one was open for 4% of the time, Pallas kernels for 0%

profile of v1, /device:TPU:0, one launch (start us, length us, event | category | flops | bytes accessed | tf_op | source)
XLA Modules:
  0.0 276.5 jit_solution(1304843077935975693)
XLA Ops:
  6.6 0.8 select_reduce_fusion.2
  7.4 1.2 fusion.48
  8.6 1.3 select_reduce_fusion.1
  9.9 2.0 fusion.50
  12.2 49.6 %all-gather.4.cloned.1.call-done = bf16[512,4096]{1,0:T(8,128)(2,1)} async-done(((bf16[64,4096]{1,0:T(8,128)(2,1)}), bf16[512,4096]{1,0:T(8,128)(2,1)}) %all-gather.4.cloned.1.call-update) | async-done | bytes 4194320 | tf_op jit(solution)/shard_map/all_gather | solution.py:38
  61.7 37.1 %while.33 = (s32[]{:T(128)}, bf16[4,128,1536]{2,1,0:T(8,128)(2,1)S(1)}, bf16[4,128,4096]{2,1,0:T(8,128)(2,1)}, s32[4]{0:T(128)S(1)}, bf16[3,4096,1536]{2,1,0:T(8,128)(2,1)}, /*index=5*/s32[]{:T(128)}, s32[]{:T(128)}, s32[]{:T(128)}) while((s32[]{:T(128)}, bf16[4,128,1536]{2,1,0:T(8,128)(2,1)S(1)}, bf16[4,128,4096]{2,1,0:T(8,128)(2,1)}, ...), condition=%wide.region_4.5_spmd, body=%wide.region_3.4_spmd.sunk | while | flops 1610809344 | bytes 14025863 | solution.py:49
  61.7 0.6 dynamic_slice.101
  64.3 6.7 %fusion.65 = bf16[4,128,1536]{2,1,0:T(8,128)(2,1)S(1)} fusion(bf16[4,128,1536]{2,1,0:T(8,128)(2,1)S(1)} %get-tuple-element.457, s32[]{:T(128)} %get-tuple-element.456, bf16[3,4096,1536]{2,1,0:T(8,128)(2,1)} %get-tuple-element.468, s32[]{:T(128)S(6)} %select_n.81, bf16[4,128,4096]{2,1,0:T(8,128)(2,1)} %get-tuple-element.466), kind=kOutput, calls=%fused_computation.6.clone.1 | convolution fusion | flops 1610809344 | bytes 14025732 | tf_op jit(solution)/shard_map/while/body/eval_jaxpr/dot_general | solution.py:47
  71.0 0.6 dynamic_slice.101
  73.5 6.7 %fusion.65 = bf16[4,128,1536]{2,1,0:T(8,128)(2,1)S(1)} fusion(bf16[4,128,1536]{2,1,0:T(8,128)(2,1)S(1)} %get-tuple-element.457, s32[]{:T(128)} %get-tuple-element.456, bf16[3,4096,1536]{2,1,0:T(8,128)(2,1)} %get-tuple-element.468, s32[]{:T(128)S(6)} %select_n.81, bf16[4,128,4096]{2,1,0:T(8,128)(2,1)} %get-tuple-element.466), kind=kOutput, calls=%fused_computation.6.clone.1 | convolution fusion | flops 1610809344 | bytes 14025732 | tf_op jit(solution)/shard_map/while/body/eval_jaxpr/dot_general | solution.py:47
  80.3 0.6 dynamic_slice.101
  82.8 6.7 %fusion.65 = bf16[4,128,1536]{2,1,0:T(8,128)(2,1)S(1)} fusion(bf16[4,128,1536]{2,1,0:T(8,128)(2,1)S(1)} %get-tuple-element.457, s32[]{:T(128)} %get-tuple-element.456, bf16[3,4096,1536]{2,1,0:T(8,128)(2,1)} %get-tuple-element.468, s32[]{:T(128)S(6)} %select_n.81, bf16[4,128,4096]{2,1,0:T(8,128)(2,1)} %get-tuple-element.466), kind=kOutput, calls=%fused_computation.6.clone.1 | convolution fusion | flops 1610809344 | bytes 14025732 | tf_op jit(solution)/shard_map/while/body/eval_jaxpr/dot_general | solution.py:47
  89.5 0.6 dynamic_slice.101
  92.1 6.7 %fusion.65 = bf16[4,128,1536]{2,1,0:T(8,128)(2,1)S(1)} fusion(bf16[4,128,1536]{2,1,0:T(8,128)(2,1)S(1)} %get-tuple-element.457, s32[]{:T(128)} %get-tuple-element.456, bf16[3,4096,1536]{2,1,0:T(8,128)(2,1)} %get-tuple-element.468, s32[]{:T(128)S(6)} %select_n.81, bf16[4,128,4096]{2,1,0:T(8,128)(2,1)} %get-tuple-element.466), kind=kOutput, calls=%fused_computation.6.clone.1 | convolution fusion | flops 1610809344 | bytes 14025732 | tf_op jit(solution)/shard_map/while/body/eval_jaxpr/dot_general | solution.py:47
  98.8 1.1 copy.14
  99.9 0.6 reshape.161
  100.6 0.9 fusion.53
  101.6 1.5 collective-permute-start
  103.1 19.1 %collective-permute-done = bf16[512,4,128]{0,2,1:T(8,128)(2,1)S(1)} collective-permute-done((bf16[512,4,128]{0,2,1:T(8,128)(2,1)S(1)}, bf16[512,4,128]{0,2,1:T(8,128)(2,1)S(1)}, u32[]{:S(2)}, u32[]{:S(2)}) %collective-permute-start) | collective-permute-done | bytes 524320 | tf_op jit(solution)/shard_map/ppermute | solution.py:75
  122.8 22.3 %collective-permute-done.1 = bf16[512,4,128]{0,2,1:T(8,128)(2,1)S(1)} collective-permute-done((bf16[512,4,128]{0,2,1:T(8,128)(2,1)S(1)}, bf16[512,4,128]{0,2,1:T(8,128)(2,1)S(1)}, u32[]{:S(2)}, u32[]{:S(2)}) %collective-permute-start.1) | collective-permute-done | bytes 524320 | tf_op jit(solution)/shard_map/ppermute | solution.py:75
  145.0 1.3 collective-permute-start.2
  146.7 1.0 copy.15
  147.7 1.1 copy.16
  148.8 8.8 %collective-permute-done.2 = bf16[512,4,128]{0,2,1:T(8,128)(2,1)} collective-permute-done((bf16[512,4,128]{0,2,1:T(8,128)(2,1)S(1)}, bf16[512,4,128]{0,2,1:T(8,128)(2,1)}, u32[]{:S(2)}, u32[]{:S(2)}) %collective-permute-start.2) | collective-permute-done | bytes 524320 | tf_op jit(solution)/shard_map/ppermute | solution.py:75
  157.6 1.1 constant_dynamic-update-slice_fusion.9
  158.9 1.1 constant_dynamic-update-slice_fusion.5
  160.3 1.6 constant_dynamic-slice_fusion.2
  161.8 3.0 %copy.17 = bf16[2048,4,128]{2,0,1:T(8,128)(2,1)S(1)} copy(bf16[2048,4,128]{0,2,1:T(8,128)(2,1)} %constant_dynamic-slice_fusion.2) | data formatting | bytes 4194304
  164.9 4.0 %copy.18 = bf16[2048,4,128]{2,0,1:T(8,128)(2,1)} copy(bf16[2048,4,128]{0,2,1:T(8,128)(2,1)} %bitcast.90) | data formatting | bytes 4194304
  168.9 23.8 %while.35 = (s32[]{:T(128)}, f32[4,4,128]{2,1,0:T(4,128)S(1)}, f32[4,128,4,128]{1,3,2,0:T(8,128)}, s32[4,128]{1,0:T(4,128)S(1)}, s32[2048]{0:T(1024)S(1)}, /*ind...) while((s32[]{:T(128)}, f32[4,4,128]{2,1,0:T(4,128)S(1)}, ...), condition=%wide.region_14.15_spmd.clone, body=%wide.region_8.14_spmd.clone.sunk | while | flops 549324416 | bytes 28503860 | solution.py:116
  168.9 0.6 fusion.69
  170.2 3.7 %conditional.3 = (f32[1,4,128]{2,1,0:T(4,128)S(1)}, f32[1,128,4,128]{3,1,2,0:T(8,128)S(1)}) conditional(s32[]{:T(128)} %convert_element_type.82, (f32[4,128]{1,0:T(4,128)S(1)}, f32[128,4,128]{2,0,1:T(8,128)S(1)}) %tuple.105, (s32[2048]{0:T(1024)S(1)}, s32[1,128]{1,0:T(1,128)S(1)}, s32[2048]{0:T(1024)S(1)}, s32[4,128]{1,0:T(4,128)S(1)}, s32[]{:T(128)}, ...), branch_computations={%region_10.10_spmd, %region_11.13_spmd} | conditional | flops 549324288 | bytes 26912820 | solution.py:114
  170.6 1.0 select_reduce_fusion
  171.6 1.2 fusion.18
  172.7 1.2 fusion.31
  174.1 0.7 constant_dynamic-update-slice_fusion.13
  174.8 0.6 fusion.69
  176.2 3.7 %conditional.3 = (f32[1,4,128]{2,1,0:T(4,128)S(1)}, f32[1,128,4,128]{3,1,2,0:T(8,128)S(1)}) conditional(s32[]{:T(128)} %convert_element_type.82, (f32[4,128]{1,0:T(4,128)S(1)}, f32[128,4,128]{2,0,1:T(8,128)S(1)}) %tuple.105, (s32[2048]{0:T(1024)S(1)}, s32[1,128]{1,0:T(1,128)S(1)}, s32[2048]{0:T(1024)S(1)}, s32[4,128]{1,0:T(4,128)S(1)}, s32[]{:T(128)}, ...), branch_computations={%region_10.10_spmd, %region_11.13_spmd} | conditional | flops 549324288 | bytes 26912820 | solution.py:114
  176.5 1.0 select_reduce_fusion
  177.5 1.2 fusion.18
  178.7 1.2 fusion.31
  180.0 0.7 constant_dynamic-update-slice_fusion.13
  180.7 0.6 fusion.69
  182.1 3.7 %conditional.3 = (f32[1,4,128]{2,1,0:T(4,128)S(1)}, f32[1,128,4,128]{3,1,2,0:T(8,128)S(1)}) conditional(s32[]{:T(128)} %convert_element_type.82, (f32[4,128]{1,0:T(4,128)S(1)}, f32[128,4,128]{2,0,1:T(8,128)S(1)}) %tuple.105, (s32[2048]{0:T(1024)S(1)}, s32[1,128]{1,0:T(1,128)S(1)}, s32[2048]{0:T(1024)S(1)}, s32[4,128]{1,0:T(4,128)S(1)}, s32[]{:T(128)}, ...), branch_computations={%region_10.10_spmd, %region_11.13_spmd} | conditional | flops 549324288 | bytes 26912820 | solution.py:114
  182.4 1.0 select_reduce_fusion
  183.4 1.2 fusion.18
  184.6 1.2 fusion.31
  185.9 0.7 constant_dynamic-update-slice_fusion.13
  186.7 0.6 fusion.69
  188.1 3.7 %conditional.3 = (f32[1,4,128]{2,1,0:T(4,128)S(1)}, f32[1,128,4,128]{3,1,2,0:T(8,128)S(1)}) conditional(s32[]{:T(128)} %convert_element_type.82, (f32[4,128]{1,0:T(4,128)S(1)}, f32[128,4,128]{2,0,1:T(8,128)S(1)}) %tuple.105, (s32[2048]{0:T(1024)S(1)}, s32[1,128]{1,0:T(1,128)S(1)}, s32[2048]{0:T(1024)S(1)}, s32[4,128]{1,0:T(4,128)S(1)}, s32[]{:T(128)}, ...), branch_computations={%region_10.10_spmd, %region_11.13_spmd} | conditional | flops 549324288 | bytes 26912820 | solution.py:114
  188.4 1.0 select_reduce_fusion
  189.4 1.2 fusion.18
  190.6 1.2 fusion.31
  191.9 0.7 constant_dynamic-update-slice_fusion.13
  192.7 1.3 divide_convert_fusion
  194.0 25.9 %while.34 = (s32[]{:T(128)}, bf16[4,128,4096]{2,1,0:T(8,128)(2,1)}, bf16[4,128,512]{1,2,0:T(8,128)(2,1)S(1)}, s32[4]{0:T(128)S(1)}, bf16[3,512,4096]{2,1,0:T(8,128)(2,1)}, /*index=5*/s32[]{:T(128)}, s32[]{:T(128)}, s32[]{:T(128)}) while((s32[]{:T(128)}, bf16[4,128,4096]{2,1,0:T(8,128)(2,1)}, bf16[4,128,512]{1,2,0:T(8,128)(2,1)S(1)}, ...), condition=%wide.region_16.17_spmd, body=%wide.region_15.16_spmd.sunk | while | flops 536870912 | bytes 6423687 | solution.py:128
  194.0 0.6 dynamic_slice.104
  196.5 3.9 %fusion.68 = bf16[4,128,4096]{2,1,0:T(8,128)(2,1)} fusion(bf16[4,128,4096]{2,1,0:T(8,128)(2,1)} %get-tuple-element.517, s32[]{:T(128)} %get-tuple-element.516, bf16[3,512,4096]{2,1,0:T(8,128)(2,1)} %get-tuple-element.528, s32[]{:T(128)S(6)} %select_n.82, bf16[4,128,512]{1,2,0:T(8,128)(2,1)S(1)} %get-tuple-element.526), kind=kOutput, calls=%fused_computation.36.clone.1 | convolution fusion | flops 536870912 | bytes 6423556 | tf_op jit(solution)/shard_map/while/body/eval_jaxpr/dot_general | solution.py:126
  200.5 0.6 dynamic_slice.104
  203.0 4.0 %fusion.68 = bf16[4,128,4096]{2,1,0:T(8,128)(2,1)} fusion(bf16[4,128,4096]{2,1,0:T(8,128)(2,1)} %get-tuple-element.517, s32[]{:T(128)} %get-tuple-element.516, bf16[3,512,4096]{2,1,0:T(8,128)(2,1)} %get-tuple-element.528, s32[]{:T(128)S(6)} %select_n.82, bf16[4,128,512]{1,2,0:T(8,128)(2,1)S(1)} %get-tuple-element.526), kind=kOutput, calls=%fused_computation.36.clone.1 | convolution fusion | flops 536870912 | bytes 6423556 | tf_op jit(solution)/shard_map/while/body/eval_jaxpr/dot_general | solution.py:126
  209.5 3.9 %fusion.68 = bf16[4,128,4096]{2,1,0:T(8,128)(2,1)} fusion(bf16[4,128,4096]{2,1,0:T(8,128)(2,1)} %get-tuple-element.517, s32[]{:T(128)} %get-tuple-element.516, bf16[3,512,4096]{2,1,0:T(8,128)(2,1)} %get-tuple-element.528, s32[]{:T(128)S(6)} %select_n.82, bf16[4,128,512]{1,2,0:T(8,128)(2,1)S(1)} %get-tuple-element.526), kind=kOutput, calls=%fused_computation.36.clone.1 | convolution fusion | flops 536870912 | bytes 6423556 | tf_op jit(solution)/shard_map/while/body/eval_jaxpr/dot_general | solution.py:126
  216.0 3.9 %fusion.68 = bf16[4,128,4096]{2,1,0:T(8,128)(2,1)} fusion(bf16[4,128,4096]{2,1,0:T(8,128)(2,1)} %get-tuple-element.517, s32[]{:T(128)} %get-tuple-element.516, bf16[3,512,4096]{2,1,0:T(8,128)(2,1)} %get-tuple-element.528, s32[]{:T(128)S(6)} %select_n.82, bf16[4,128,512]{1,2,0:T(8,128)(2,1)S(1)} %get-tuple-element.526), kind=kOutput, calls=%fused_computation.36.clone.1 | convolution fusion | flops 536870912 | bytes 6423556 | tf_op jit(solution)/shard_map/while/body/eval_jaxpr/dot_general | solution.py:126
  219.9 48.1 %reduce-scatter.2.cloned.1.call-done = bf16[64,4096]{1,0:T(8,128)(2,1)} async-done(((bf16[512,4096]{1,0:T(8,128)(2,1)}), bf16[64,4096]{1,0:T(8,128)(2,1)}) %reduce-scatter.2.cloned.1.call-update) | async-done | bytes 524304 | tf_op jit(solution)/shard_map/reduce_scatter | solution.py:131
  268.0 2.0 fusion.51
  (87 shorter events, 4.8 us)
Async XLA Ops:
  6.5 5.5 %copy-start.2 = (s32[16]{0:T(128)S(1)}, s32[16]{0:T(128)}, u32[]{:S(2)}) copy-start(s32[16]{0:T(128)} %param.18) | copy-start | bytes 196
  6.5 55.2 %all-gather.4.cloned.1.call-start = ((), (), s32[]{:S(2)}) async-start(), calls=%async_computation.1 | async-start | bytes 4718592 | tf_op jit(solution)/shard_map/all_gather | solution.py:38
  12.0 152.9 %all-gather.6.cloned.1.call-start = ((), (), s32[]{:S(2)}) async-start(), calls=%async_computation.3 | async-start | bytes 2621440 | tf_op jit(solution)/shard_map/all_gather | solution.py:79
  99.9 46.4 %copy-start.3 = (s32[4]{0:T(128)S(1)}, s32[4]{0:T(128)}, u32[]{:S(2)}) copy-start(s32[4]{0:T(128)} %param.19) | copy-start | bytes 52
  101.5 166.5 %reduce-scatter.2.cloned.1.call-start = ((), (), s32[]{:S(2)}) async-start(), calls=%async_computation.2 | async-start | bytes 4718592 | tf_op jit(solution)/shard_map/reduce_scatter | solution.py:131
  101.6 20.6 %collective-permute-start = (bf16[512,4,128]{0,2,1:T(8,128)(2,1)S(1)}, bf16[512,4,128]{0,2,1:T(8,128)(2,1)S(1)}, u32[]{:S(2)}, u32[]{:S(2)}) collective-permute-start(bf16[512,4,128]{0,2,1:T(8,128)(2,1)S(1)} %get-tuple-element.317), channel_id=1, source_target_pairs={{0,8},{8,16},{16,24},{24,0},{1,9},{9,17},{17,25},{25,1},{2,10},{10... | collective-permute-start | bytes 1572872 | tf_op jit(solution)/shard_map/ppermute | solution.py:75
  122.2 22.8 %collective-permute-start.1 = (bf16[512,4,128]{0,2,1:T(8,128)(2,1)S(1)}, bf16[512,4,128]{0,2,1:T(8,128)(2,1)S(1)}, u32[]{:S(2)}, u32[]{:S(2)}) collective-permute-start(bf16[512,4,128]{0,2,1:T(8,128)(2,1)S(1)} %collective-permute-done), channel_id=1, source_target_pairs={{0,8},{8,16},{16,24},{24,0},{1,9},{9,17},{17,25},{25,1},{2,10},{10... | collective-permute-start | bytes 1572872 | tf_op jit(solution)/shard_map/ppermute | solution.py:75
  145.0 12.5 %collective-permute-start.2 = (bf16[512,4,128]{0,2,1:T(8,128)(2,1)S(1)}, bf16[512,4,128]{0,2,1:T(8,128)(2,1)}, u32[]{:S(2)}, u32[]{:S(2)}) collective-permute-start(bf16[512,4,128]{0,2,1:T(8,128)(2,1)S(1)} %collective-permute-done.1), channel_id=1, source_target_pairs={{0,8},{8,16},{16,24},{24,0},{1,9},{9,17},{17,25},{25,1},{2,10},{10... | collective-permute-start | bytes 1572872 | tf_op jit(solution)/shard_map/ppermute | solution.py:75
  170.6 2.2 copy-start.1
  176.5 2.2 copy-start.1
  182.4 2.2 copy-start.1
  188.4 2.2 copy-start.1
  219.9 48.1 %copy-start = (bf16[64,4096]{1,0:T(8,128)(2,1)S(1)}, bf16[64,4096]{1,0:T(8,128)(2,1)}, u32[]{:S(2)}) copy-start(bf16[64,4096]{1,0:T(8,128)(2,1)} %param.14) | copy-start | bytes 1572868
Sparse Core Ops, SparseCore 0:
  12.1 49.5 all-gather.3
  101.7 47.1 all-gather.5
  220.1 47.9 reduce-scatter.1
